TPU v7x, 256 devices: a whole 4x4x8 slice. The times are simulated.
256 devices in a mesh: gz: 64 (over z, x, core), gy: 4 (over y).
Axes of the slice: x: 4, y: 4, z: 8, core: 2. Of those that a mesh axis runs over, the one named last changes fastest.
Arguments:
- iterate: float32 [128, 256, 1024], P('gz', 'gy'), may hold values from -1.5 to 1.5
- basis: bfloat16 [32, 128, 256, 1024], P(None, 'gz', 'gy'), may hold values from -6 to 6
- coeffs: float32 [32], replicated, may hold values from -0.3125 to 0.3125
- rhs: float32 [128, 256, 1024], P('gz', 'gy'), may hold values from -8 to 8
- kappa: float32 [128, 256, 1024], P('gz', 'gy'), may hold values from 0.5 to 4
- offsets: int32 [128, 256, 8], P('gz', 'gy'), may hold values from 0 to 2047
- flips: int32 [128, 256, 8], P('gz', 'gy'), may hold values from 0 to 1
Outputs:
- new_iterate: float32 [128, 256, 1024], P('gz', 'gy')
- residual: float32 [128, 256, 1024], P('gz', 'gy')
- sketch_unit: float32 [2048], replicated
All inputs are finite; a program needn't handle non-finite values.
Results may differ from a plain program's by a relative error of at most 0.00058.
Values sent between devices are 32-bit elements; how exact they have to be, the bound alone decides.
No kernel may reach another device: no remote copies, remote signals or barrier semaphores. Data moves between devices by JAX's collectives and lax.ppermute only.
A program may use at most 64 MiB of HBM per device.

v0:
```python
import jax
import jax.numpy as jnp
from jax import lax
from jax.sharding import Mesh
from jax.sharding import PartitionSpec as P

SK = 2048
BLK = 128
GZ_GY = ("gz_0", "gz_1", "gz_2", "gy")
GZ = ("gz_0", "gz_1", "gz_2")


def extended(value, sides, width):
    edges = {}
    for axis, dim in sides:
        peers, length = (lax.axis_size(axis), value.shape[dim])
        up = [(i, (i + 1) % peers) for i in range(peers - 1)]
        last = lax.slice_in_dim(value, length - width, length, axis=dim)
        initial = lax.slice_in_dim(value, 0, width, axis=dim)
        edges[dim] = (
            lax.ppermute(last, axis, up),
            lax.ppermute(initial, axis, [(b, a) for a, b in up]),
        )
    done = []
    for _, dim in sides:
        low, high = edges[dim]
        around = [(width, width) if d in done else (0, 0) for d in range(value.ndim)]
        value = jnp.concatenate([jnp.pad(low, around), value, jnp.pad(high, around)], axis=dim)
        done.append(dim)
    return value


def one_axis_at_a_time(value, axes):
    for axis in axes:
        value = lax.psum(value, axis)
    return value


def apply_operator(upad, kpad):
    field = upad[1:-1, 1:-1, :]
    coef = kpad[1:-1, 1:-1, :]
    total = 0.05 * field
    neighbours = [
        (upad[2:, 1:-1, :], kpad[2:, 1:-1, :]),
        (upad[:-2, 1:-1, :], kpad[:-2, 1:-1, :]),
        (upad[1:-1, 2:, :], kpad[1:-1, 2:, :]),
        (upad[1:-1, :-2, :], kpad[1:-1, :-2, :]),
    ]
    zero_col = jnp.zeros_like(field[:, :, :1])
    neighbours.append(
        (
            jnp.concatenate([field[:, :, 1:], zero_col], 2),
            jnp.concatenate([coef[:, :, 1:], zero_col], 2),
        )
    )
    neighbours.append(
        (
            jnp.concatenate([zero_col, field[:, :, :-1]], 2),
            jnp.concatenate([zero_col, coef[:, :, :-1]], 2),
        )
    )
    for other, kother in neighbours:
        total = total + 0.5 * (coef + kother) * (field - other)
    return total


def local_sketch(residual, offsets, flips):
    blocks = residual.reshape(-1, BLK)
    signs = (2 * flips - 1).astype(jnp.float32).reshape(-1, 1)
    columns = lax.broadcasted_iota(jnp.int32, (1, SK), 1)
    placed = jnp.where(offsets.reshape(-1, 1) == columns, signs, 0.0)
    spread = jnp.dot(
        blocks.T, placed, precision=lax.Precision.HIGHEST, preferred_element_type=jnp.float32
    )
    doubled = jnp.concatenate([spread, spread], 1).reshape(-1)
    doubled = jnp.concatenate([doubled, jnp.zeros((SK,), jnp.float32)])
    skewed = doubled[SK : SK + BLK * (2 * SK - 1)].reshape(BLK, 2 * SK - 1)
    return jnp.sum(skewed[:, :SK], axis=0)


def shards(iterate, basis, coeffs, rhs, kappa, offsets, flips):
    coeff_b = coeffs.astype(jnp.bfloat16)
    new_iterate = iterate + jnp.einsum(
        "k,kzyx->zyx", coeff_b, basis, preferred_element_type=jnp.float32
    )
    stacked = jnp.stack([new_iterate, kappa])
    padded = extended(stacked, ((GZ, 1), ("gy", 2)), 1)
    upad = padded[0]
    kpad = padded[1]
    residual = rhs - apply_operator(upad, kpad)
    partial_sketch = local_sketch(residual, offsets, flips)
    sketch = one_axis_at_a_time(partial_sketch, GZ_GY)
    sketch_unit = sketch / jnp.sqrt(jnp.mean(sketch * sketch) + 1e-06)
    return (new_iterate, residual, sketch_unit)


def solution(mesh):
    finer = Mesh(mesh.devices.reshape(8, 4, 2, mesh.shape["gy"]), ("gz_0", "gz_1", "gz_2", "gy"))
    placed = (
        P(GZ, "gy", None),
        P(None, GZ, "gy", None),
        P(),
        P(GZ, "gy", None),
        P(GZ, "gy", None),
        P(GZ, "gy", None),
        P(GZ, "gy", None),
    )
    return jax.shard_map(
        shards,
        mesh=finer,
        in_specs=placed,
        out_specs=(P(GZ, "gy", None), P(GZ, "gy", None), P()),
        check_vma=False,
    )
```

profile of v0, /device:TPU:1, one launch (start us, length us, event | category | flops | bytes accessed | tf_op | source)
XLA Modules:
  0.0 84.5 jit_solution(9888327381164182605)
XLA Ops:
  0.6 0.0 copy-start.3
  0.6 0.0 copy-start.1
  0.7 12.6 %fusion = f32[1,2,64,1024]{3,0,2,1:T(1,128)S(1)} fusion(bf16[32,2,64,1024]{3,2,1,0:T(8,128)(2,1)} %param.8, f32[32]{0:T(128)} %param.9), kind=kOutput, calls=%fused_computation | convolution fusion | flops 8388640 | bytes 8913024 | tf_op jit(solution)/shard_map/k,kzyx->zyx/dot_general | solution.py:83
  13.2 0.0 copy-done.3
  13.2 0.0 copy-start.6
  13.2 0.0 copy-start.5
  13.2 0.1 bitcast_add_fusion
  13.4 0.0 copy-start
  13.4 0.0 copy-done.1
  13.4 0.1 fusion.8
  13.5 4.5 %collective-permute-start.1 = (f32[2,1,64,1024]{3,2,1,0:T(8,128)S(1)}, f32[2,1,64,1024]{3,2,1,0:T(8,128)S(1)}, u32[]{:S(2)}, u32[]{:S(2)}) collective-permute-start(f32[2,1,64,1024]{3,2,1,0:T(8,128)S(1)} %get-tuple-element.9), channel_id=1, source_target_pairs={{0,4},{4,8},{8,12},{12,16},{16,20},{20,24},{24,28},{28,32},{32,36}... | collective-permute-start | bytes 1572872 | tf_op jit(solution)/shard_map/ppermute | solution.py:21
  18.0 1.9 %collective-permute-start.2 = (f32[2,1,64,1024]{3,2,1,0:T(8,128)S(1)}, f32[2,1,64,1024]{3,2,1,0:T(8,128)S(1)}, u32[]{:S(2)}, u32[]{:S(2)}) collective-permute-start(f32[2,1,64,1024]{3,2,1,0:T(8,128)S(1)} %get-tuple-element.10), channel_id=1, source_target_pairs={{4,0},{8,4},{12,8},{16,12},{20,16},{24,20},{28,24},{32,28},{36,32}... | collective-permute-start | bytes 1572872 | tf_op jit(solution)/shard_map/ppermute | solution.py:22
  20.0 3.2 %collective-permute-start = (f32[2,2,1,1024]{3,2,1,0:T(1,128)S(1)}, f32[2,2,1,1024]{3,2,1,0:T(1,128)S(1)}, u32[]{:S(2)}, u32[]{:S(2)}) collective-permute-start(f32[2,2,1,1024]{3,2,1,0:T(1,128)S(1)} %get-tuple-element.11), channel_id=1, source_target_pairs={{0,1},{1,2},{2,3},{4,5},{5,6},{6,7},{8,9},{9,10},{10,11},{12,13},{... | collective-permute-start | bytes 49160 | tf_op jit(solution)/shard_map/ppermute | solution.py:21
  23.2 1.5 %collective-permute-start.3 = (f32[2,2,1,1024]{3,2,1,0:T(1,128)S(1)}, f32[2,2,1,1024]{3,2,1,0:T(1,128)S(1)}, u32[]{:S(2)}, u32[]{:S(2)}) collective-permute-start(f32[2,2,1,1024]{3,2,1,0:T(1,128)S(1)} %get-tuple-element.12), channel_id=1, source_target_pairs={{1,0},{2,1},{3,2},{5,4},{6,5},{7,6},{9,8},{10,9},{11,10},{13,12},{... | collective-permute-start | bytes 49160 | tf_op jit(solution)/shard_map/ppermute | solution.py:22
  24.7 0.0 copy-done.6
  24.7 0.1 copy.13
  24.8 0.1 broadcast_in_dim.16
  24.9 0.0 copy-done.5
  24.9 0.1 copy.12
  25.0 0.1 eq.15
  25.1 0.0 collective-permute-done
  25.1 2.6 %collective-permute-done.3 = f32[2,2,1,1024]{3,2,1,0:T(1,128)S(1)} collective-permute-done((f32[2,2,1,1024]{3,2,1,0:T(1,128)S(1)}, f32[2,2,1,1024]{3,2,1,0:T(1,128)S(1)}, u32[]{:S(2)}, u32[]{:S(2)}) %collective-permute-start.3) | collective-permute-done | bytes 16416 | tf_op jit(solution)/shard_map/ppermute | solution.py:22
  27.7 0.0 collective-permute-done.1
  27.7 0.8 collective-permute-done.2
  28.5 0.3 select_maximum_fusion
  28.8 0.0 copy-done
  28.8 0.2 slice_bitcast_fusion
  29.0 0.0 copy-start.4
  29.0 0.5 fusion.27
  29.5 0.6 copy-done.4
  30.0 0.8 fusion.13
  30.8 0.0 copy-start.2
  30.9 0.1 reshape.19
  30.9 5.4 %fusion.2 = f32[128,2048]{1,0:T(8,128)S(1)} fusion(f32[1024,128]{1,0:T(8,128)S(1)} %reshape.19, f32[1024]{0:T(1024)S(1)} %broadcast_in_dim.16, s32[1024]{0:T(1024)S(1)} %eq.15), kind=kOutput, calls=%fused_computation.2 | convolution fusion | flops 3225419776 | bytes 1581056 | tf_op jit(solution)/shard_map/dot_general | solution.py:72
  36.4 0.0 copy-done.2
  36.4 0.2 maximum_bitcast_fusion
  36.6 0.4 copy.17
  37.0 0.1 pad_slice_fusion
  37.2 2.5 %reshape.21 = f32[128,4095]{1,0:T(8,128)} reshape(f32[524160]{0:T(1024)S(1)} %pad_slice_fusion) | data formatting | bytes 4193280 | tf_op jit(solution)/shard_map/reshape | solution.py:77
  39.6 1.3 %slice_reduce_fusion = f32[2048]{0:T(1024)S(1)} fusion(f32[128,4095]{1,0:T(8,128)} %reshape.21), kind=kLoop, calls=%fused_computation.20 | loop fusion | flops 260096 | bytes 1056768 | tf_op jit(solution)/shard_map/reduce_sum | solution.py:78
  40.9 16.7 %psum.28 = f32[2048]{0:T(1024)S(1)} all-reduce(f32[2048]{0:T(1024)S(1)} %slice_reduce_fusion), channel_id=1, replica_groups=mesh['gz_0'=8,'gz_1'=4,'gz_2'=2,'gy'=4] {'gz_0'}, use_global_device_ids=true, to_apply=%region_1.2 | all-reduce | flops 2048 | bytes 16384 | tf_op jit(solution)/shard_map/psum | solution.py:35
  57.6 10.0 %psum.29 = f32[2048]{0:T(1024)S(1)} all-reduce(f32[2048]{0:T(1024)S(1)} %psum.28), channel_id=1, replica_groups=mesh['gz_0'=8,'gz_1'=4,'gz_2'=2,'gy'=4] {'gz_1'}, use_global_device_ids=true, to_apply=%region_2.3 | all-reduce | flops 2048 | bytes 16384 | tf_op jit(solution)/shard_map/psum | solution.py:35
  67.7 7.5 %psum.30 = f32[2048]{0:T(1024)S(1)} all-reduce(f32[2048]{0:T(1024)S(1)} %psum.29), channel_id=1, replica_groups=mesh['gz_0'=8,'gz_1'=4,'gz_2'=2,'gy'=4] {'gz_2'}, use_global_device_ids=true, to_apply=%region_3.4 | all-reduce | flops 2048 | bytes 16384 | tf_op jit(solution)/shard_map/psum | solution.py:35
  75.2 7.4 %psum.31 = f32[2048]{0:T(1024)S(1)} all-reduce(f32[2048]{0:T(1024)S(1)} %psum.30), channel_id=1, replica_groups=mesh['gz_0'=8,'gz_1'=4,'gz_2'=2,'gy'=4] {'gy'}, use_global_device_ids=true, to_apply=%region_4.5 | all-reduce | flops 2048 | bytes 16384 | tf_op jit(solution)/shard_map/psum | solution.py:35
  82.6 0.6 multiply_reduce_fusion
  83.9 0.6 broadcast_divide_fusion
  (2 shorter events, 0.0 us)
Async XLA Ops:
  0.6 12.6 %copy-start.3 = (f32[2,64,1024]{2,1,0:T(8,128)S(1)}, f32[2,64,1024]{2,1,0:T(8,128)}, u32[]{:S(2)}) copy-start(f32[2,64,1024]{2,1,0:T(8,128)} %param.7) | copy-start | bytes 1572868
  0.6 12.7 %copy-start.1 = (f32[2,64,1024]{2,1,0:T(8,128)S(1)}, f32[2,64,1024]{2,1,0:T(8,128)}, u32[]{:S(2)}) copy-start(f32[2,64,1024]{2,1,0:T(8,128)} %param.11) | copy-start | bytes 1572868
  13.2 11.4 %copy-start.6 = (s32[2,64,8]{1,2,0:T(8,128)S(1)}, s32[2,64,8]{1,2,0:T(8,128)}, u32[]{:S(2)}) copy-start(s32[2,64,8]{1,2,0:T(8,128)} %param.13) | copy-start | bytes 12292
  13.2 11.6 %copy-start.5 = (s32[2,64,8]{1,2,0:T(8,128)S(1)}, s32[2,64,8]{1,2,0:T(8,128)}, u32[]{:S(2)}) copy-start(s32[2,64,8]{1,2,0:T(8,128)} %param.12) | copy-start | bytes 12292
  13.4 15.5 %copy-start = (f32[2,64,1024]{2,1,0:T(8,128)}, f32[2,64,1024]{2,1,0:T(8,128)S(1)}, u32[]{:S(2)}) copy-start(f32[2,64,1024]{2,1,0:T(8,128)S(1)} %bitcast_add_fusion) | copy-start | bytes 1572868
  13.5 14.2 %collective-permute-start.1 = (f32[2,1,64,1024]{3,2,1,0:T(8,128)S(1)}, f32[2,1,64,1024]{3,2,1,0:T(8,128)S(1)}, u32[]{:S(2)}, u32[]{:S(2)}) collective-permute-start(f32[2,1,64,1024]{3,2,1,0:T(8,128)S(1)} %get-tuple-element.9), channel_id=1, source_target_pairs={{0,4},{4,8},{8,12},{12,16},{16,20},{20,24},{24,28},{28,32},{32,36}... | collective-permute-start | bytes 1572872 | tf_op jit(solution)/shard_map/ppermute | solution.py:21
  18.0 10.5 %collective-permute-start.2 = (f32[2,1,64,1024]{3,2,1,0:T(8,128)S(1)}, f32[2,1,64,1024]{3,2,1,0:T(8,128)S(1)}, u32[]{:S(2)}, u32[]{:S(2)}) collective-permute-start(f32[2,1,64,1024]{3,2,1,0:T(8,128)S(1)} %get-tuple-element.10), channel_id=1, source_target_pairs={{4,0},{8,4},{12,8},{16,12},{20,16},{24,20},{28,24},{32,28},{36,32}... | collective-permute-start | bytes 1572872 | tf_op jit(solution)/shard_map/ppermute | solution.py:22
  20.0 5.1 %collective-permute-start = (f32[2,2,1,1024]{3,2,1,0:T(1,128)S(1)}, f32[2,2,1,1024]{3,2,1,0:T(1,128)S(1)}, u32[]{:S(2)}, u32[]{:S(2)}) collective-permute-start(f32[2,2,1,1024]{3,2,1,0:T(1,128)S(1)} %get-tuple-element.11), channel_id=1, source_target_pairs={{0,1},{1,2},{2,3},{4,5},{5,6},{6,7},{8,9},{9,10},{10,11},{12,13},{... | collective-permute-start | bytes 49160 | tf_op jit(solution)/shard_map/ppermute | solution.py:21
  23.2 4.5 %collective-permute-start.3 = (f32[2,2,1,1024]{3,2,1,0:T(1,128)S(1)}, f32[2,2,1,1024]{3,2,1,0:T(1,128)S(1)}, u32[]{:S(2)}, u32[]{:S(2)}) collective-permute-start(f32[2,2,1,1024]{3,2,1,0:T(1,128)S(1)} %get-tuple-element.12), channel_id=1, source_target_pairs={{1,0},{2,1},{3,2},{5,4},{6,5},{7,6},{9,8},{10,9},{11,10},{13,12},{... | collective-permute-start | bytes 49160 | tf_op jit(solution)/shard_map/ppermute | solution.py:22
  29.0 1.0 %copy-start.4 = (f32[2,64,1024]{2,1,0:T(8,128)S(1)}, f32[2,64,1024]{2,1,0:T(8,128)}, u32[]{:S(2)}) copy-start(f32[2,64,1024]{2,1,0:T(8,128)} %param.10) | copy-start | bytes 1572868
  30.8 5.5 %copy-start.2 = (f32[2,64,1024]{2,1,0:T(8,128)}, f32[2,64,1024]{2,1,0:T(8,128)S(1)}, u32[]{:S(2)}) copy-start(f32[2,64,1024]{2,1,0:T(8,128)S(1)} %fusion.13) | copy-start | bytes 1572868
where the time goes:
time: 85.6 us; the launch traced here: 84.5 us
  blocking collectives  41.6 us (49%)
  matrix products  18 us (21%)
  starting transfers between devices  11.1 us (13%)
  local copies, waits for them, and re-layouts  4.64 us (5%)
  other arithmetic  4.1 us (5%)
  waiting for transfers between devices  3.42 us (4%)
  between operations  1.59 us (2%)
    psum x4, blocking collectives, one_axis_at_a_time(): value = lax.psum(value, axis)  41.6 us
    dot_general x1, matrix products, shards(): jnp.einsum('k,kzyx->zyx', coeff_b, basis, preferred_element_type=jnp.floa...  12.6 us
    ppermute x2, starting transfers between devices, extended(): lax.ppermute(last, axis, up)  7.69 us
    dot_general x1, matrix products, local_sketch(): jnp.dot(blocks.T, placed, precision=lax.Precision.HIGHEST, preferred_elem...  5.44 us
    ppermute x2, waiting for transfers between devices, extended(): lax.ppermute(initial, axis, [(b, a) for a, b in up])  3.41 us
    ppermute x2, starting transfers between devices, extended(): lax.ppermute(initial, axis, [(b, a) for a, b in up])  3.41 us
    reshape x1, local copies, waits for them, and re-layouts, local_sketch(): skewed = doubled[SK:SK + BLK * (2 * SK - 1)].reshape(BLK, 2 * SK - 1)  2.47 us
  transfers between devices with their start and end apart: 4, of which 2 were waited for; matrix products, arithmetic and copies ran while one was open for 0% of the time, Pallas kernels for 0%

commit v1 on v0

v1 whole, which is shorter than its diff:
```python
import functools

import jax
import jax.numpy as jnp
from jax import lax
from jax.experimental import pallas as pl
from jax.experimental.pallas import tpu as pltpu
from jax.sharding import Mesh
from jax.sharding import PartitionSpec as P

SK = 2048
BLK = 128
ROWS = SK // BLK
GZ = ("z", "x", "core")
CHUNK = 16


def stream_kernel(coeff_ref, iterate_ref, basis_ref, new_ref, same_ref, cross_ref, ye_ref, yo_ref, held, splat, sems):
    kb, nz, ny, nx = basis_ref.shape
    pieces = ny // CHUNK
    copies = []
    for i in range(pieces):
        rows = pl.ds(i * CHUNK, CHUNK)
        copies.append(pltpu.make_async_copy(basis_ref.at[:, :, rows, :], held.at[i], sems.at[i]))
    for copy in copies:
        copy.start()
    core = lax.axis_index("core")
    odd = lax.rem(lax.axis_index("gy"), 2)
    rounded = coeff_ref[...].astype(jnp.bfloat16).astype(jnp.float32)
    for k in range(kb):
        splat[k] = jnp.broadcast_to(rounded[:, k : k + 1], (8, BLK))
    for i in range(pieces):
        copies[i].wait()

        @pl.loop(0, nx // BLK)
        def _(j, i=i):
            lanes = pl.ds(pl.multiple_of(j * BLK, BLK), BLK)
            rows = pl.ds(i * CHUNK, CHUNK)
            acc = [iterate_ref[z, rows, lanes] for z in range(nz)]
            for k in range(kb):
                scale = splat[k]
                scale = jnp.concatenate([scale] * (CHUNK // 8), 0)
                for z in range(nz):
                    acc[z] = acc[z] + scale * held[i, k, z, :, lanes].astype(jnp.float32)
            for z in range(nz):
                new_ref[z, rows, lanes] = acc[z]
            same_ref[rows, lanes] = jnp.where(core == 0, acc[1], acc[0])
            cross_ref[rows, lanes] = jnp.where(core == 0, acc[0], acc[1])

    for z in range(nz):
        low, high = new_ref[z, 0:1, :], new_ref[z, ny - 1 : ny, :]
        ye_ref[z : z + 1, :] = jnp.where(odd == 0, high, low)
        yo_ref[z : z + 1, :] = jnp.where(odd == 0, low, high)


def update(coeffs, iterate, basis):
    kb, nz, ny, nx = basis.shape
    vmem = pl.BlockSpec(memory_space=pltpu.VMEM)
    plane = jax.ShapeDtypeStruct((ny, nx), jnp.float32)
    row = jax.ShapeDtypeStruct((nz, nx), jnp.float32)
    return pl.pallas_call(
        stream_kernel,
        out_shape=(jax.ShapeDtypeStruct(iterate.shape, jnp.float32), plane, plane, row, row),
        in_specs=[vmem, vmem, pl.BlockSpec(memory_space=pl.ANY)],
        out_specs=(vmem,) * 5,
        scratch_shapes=[
            pltpu.VMEM((ny // CHUNK, kb, nz, CHUNK, nx), jnp.bfloat16),
            pltpu.VMEM((kb, 8, BLK), jnp.float32),
            pltpu.SemaphoreType.DMA((ny // CHUNK,)),
        ],
        compiler_params=pltpu.CompilerParams(vmem_limit_bytes=16 << 20),
        cost_estimate=pl.CostEstimate(flops=2 * basis.size, bytes_accessed=2 * basis.size, transcendentals=0),
        name="update",
    )(coeffs.reshape(1, kb), iterate, basis)


def shifted(value, by, axis):
    return pltpu.roll(value, by % value.shape[axis], axis)


def residual_kernel(
    u_ref, k_ref, rhs_ref, off_ref, flip_ref,
    us_ref, uc_ref, ks_ref, kc_ref, ue_ref, uo_ref, ke_ref, ko_ref,
    res_ref, part_ref,
):
    nz, ny, nx = u_ref.shape
    core = lax.axis_index("core")
    odd = lax.rem(lax.axis_index("gy"), 2)
    lane = lax.broadcasted_iota(jnp.int32, (8, nx), 1)
    line = lax.broadcasted_iota(jnp.int32, (8, nx), 0)
    first, last = lane == 0, lane == nx - 1
    top, bottom = line == 0, line == 7

    def pick(even, same, cross):
        return jnp.where(even, same, cross)

    for z in range(nz):
        lowy_u = pick(odd == 0, uo_ref[z : z + 1, :], ue_ref[z : z + 1, :])
        lowy_k = pick(odd == 0, ko_ref[z : z + 1, :], ke_ref[z : z + 1, :])
        highy_u = pick(odd == 0, ue_ref[z : z + 1, :], uo_ref[z : z + 1, :])
        highy_k = pick(odd == 0, ke_ref[z : z + 1, :], ko_ref[z : z + 1, :])
        for y in range(0, ny, 8):
            rows = slice(y, y + 8)
            u, k = u_ref[z, rows, :], k_ref[z, rows, :]
            total = 0.05 * u
            halo = core == (0 if z else 1)
            uz = pick(halo, us_ref[rows, :], uc_ref[rows, :])
            kz = pick(halo, ks_ref[rows, :], kc_ref[rows, :])
            total = total + 0.5 * (k + kz) * (u - uz)
            total = total + 0.5 * (k + k_ref[1 - z, rows, :]) * (u - u_ref[1 - z, rows, :])
            if y == 0:
                ul = jnp.where(top, lowy_u, shifted(u, 1, 0))
                kl = jnp.where(top, lowy_k, shifted(k, 1, 0))
            else:
                ul, kl = u_ref[z, y - 1 : y + 7, :], k_ref[z, y - 1 : y + 7, :]
            if y == ny - 8:
                uh = jnp.where(bottom, highy_u, shifted(u, -1, 0))
                kh = jnp.where(bottom, highy_k, shifted(k, -1, 0))
            else:
                uh, kh = u_ref[z, y + 1 : y + 9, :], k_ref[z, y + 1 : y + 9, :]
            total = total + 0.5 * (k + kl) * (u - ul)
            total = total + 0.5 * (k + kh) * (u - uh)
            ur = jnp.where(last, 0.0, shifted(u, -1, 1))
            kr = jnp.where(last, 0.0, shifted(k, -1, 1))
            right = 0.5 * (k + kr) * (u - ur)
            left = jnp.where(first, -0.5 * k * u, shifted(right, 1, 1))
            res_ref[z, rows, :] = rhs_ref[z, rows, :] - (total + (right - left))

    spot = lax.broadcasted_iota(jnp.int32, (ny, BLK), 1)
    slot = lax.broadcasted_iota(jnp.int32, (ROWS, ny), 0)
    whole = jnp.zeros((ROWS, BLK), jnp.float32)
    carry = jnp.zeros((ROWS, BLK), jnp.float32)
    for z in range(nz):
        turned = jnp.transpose(off_ref[z] & (BLK - 1))
        for q in range(nx // BLK):
            by = jnp.broadcast_to(turned[:, q : q + 1], (ny, BLK))
            block = res_ref[z, :, q * BLK : (q + 1) * BLK]
            block = jnp.take_along_axis(block, (spot - by) & (BLK - 1), axis=1)
            high = block.astype(jnp.bfloat16)
            low = (block - high.astype(jnp.float32)).astype(jnp.bfloat16)
            sign = (2 * flip_ref[z, q : q + 1, :] - 1).astype(jnp.float32)
            row = jnp.right_shift(off_ref[z, q : q + 1, :], 7)
            place = jnp.where(slot == row, sign, 0.0).astype(jnp.bfloat16)
            here = spot >= by
            none = jnp.zeros_like(high)
            for term in (high, low):
                pair = jnp.concatenate([jnp.where(here, term, none), jnp.where(here, none, term)], 1)
                got = jnp.dot(place, pair, preferred_element_type=jnp.float32)
                whole = whole + got[:, :BLK]
                carry = carry + got[:, BLK:]
    sketch = whole + jnp.concatenate([carry[ROWS - 1 :], carry[: ROWS - 1]], 0)
    for m in range(part_ref.shape[0]):
        part_ref[m] = sketch


def residual_and_sketch(members, *arrays):
    vmem = pl.BlockSpec(memory_space=pltpu.VMEM)
    u = arrays[0]
    return pl.pallas_call(
        residual_kernel,
        out_shape=(
            jax.ShapeDtypeStruct(u.shape, jnp.float32),
            jax.ShapeDtypeStruct((members, ROWS, BLK), jnp.float32),
        ),
        in_specs=[vmem] * len(arrays),
        out_specs=(vmem, vmem),
        compiler_params=pltpu.CompilerParams(vmem_limit_bytes=16 << 20),
        cost_estimate=pl.CostEstimate(flops=60 * u.size, bytes_accessed=8 * u.size, transcendentals=0),
        name="residual",
    )(*arrays)


def scale_kernel(parts_ref, out_ref):
    sketch = jnp.sum(parts_ref[...], axis=0)
    mean = jnp.sum(sketch * sketch) * (1.0 / SK)
    out_ref[...] = sketch / jnp.sqrt(jnp.broadcast_to(mean + 1e-06, sketch.shape))


def scaled(parts):
    vmem = pl.BlockSpec(memory_space=pltpu.VMEM)
    return pl.pallas_call(
        scale_kernel,
        out_shape=jax.ShapeDtypeStruct((ROWS, BLK), jnp.float32),
        in_specs=[vmem],
        out_specs=vmem,
        compiler_params=pltpu.CompilerParams(vmem_limit_bytes=4 << 20),
        name="scaled",
    )(parts)


def shards(sizes, iterate, basis, coeffs, rhs, kappa, offsets, flips):
    gz = sizes["z"] * sizes["x"] * sizes["core"]
    gy = sizes["gy"]
    core = lax.axis_index("core")
    odd = lax.rem(lax.axis_index("gy"), 2)
    same = [(i, i ^ 1) for i in range(gz)]
    cross = [(i, i + 1) for i in range(1, gz - 1, 2)] + [(i + 1, i) for i in range(1, gz - 1, 2)]
    even_y = [(i, i ^ 1) for i in range(gy)]
    odd_y = [(i, i + 1) for i in range(1, gy - 1, 2)] + [(i + 1, i) for i in range(1, gy - 1, 2)]

    k_cross = lax.ppermute(jnp.where(core == 0, kappa[0], kappa[1]), GZ, cross)
    k_same = lax.ppermute(jnp.where(core == 0, kappa[1], kappa[0]), GZ, same)
    k_even = lax.ppermute(jnp.where(odd == 0, kappa[:, -1], kappa[:, 0]), "gy", even_y)
    k_odd = lax.ppermute(jnp.where(odd == 0, kappa[:, 0], kappa[:, -1]), "gy", odd_y)

    u, u_same, u_cross, u_even, u_odd = update(coeffs, iterate, basis)
    u_cross = lax.ppermute(u_cross, GZ, cross)
    u_same = lax.ppermute(u_same, GZ, same)
    u_even = lax.ppermute(u_even, "gy", even_y)
    u_odd = lax.ppermute(u_odd, "gy", odd_y)

    plane_of = ("x", "gy")
    line_of = ("z", "core")
    members = sizes["x"] * sizes["gy"]
    others = sizes["z"] * sizes["core"]
    residual, part = residual_and_sketch(
        members, u, kappa, rhs, jnp.swapaxes(offsets, 1, 2), jnp.swapaxes(flips, 1, 2),
        u_same, u_cross, k_same, k_cross, u_even, u_odd, k_even, k_odd,
    )
    part = lax.all_to_all(part, plane_of, 0, 0)
    part = jnp.broadcast_to(jnp.sum(part, 0), (others, ROWS, BLK))
    part = lax.all_to_all(part, line_of, 0, 0)
    return u, residual, scaled(part).reshape(SK)


def build(mesh, outer):
    gy = mesh.shape["gy"]
    finer = Mesh(mesh.devices.reshape(*outer, gy), (*GZ, "gy"))
    sizes = dict(finer.shape)
    field = P(GZ, "gy", None)
    return jax.shard_map(
        functools.partial(shards, sizes),
        mesh=finer,
        in_specs=(field, P(None, GZ, "gy", None), P(), field, field, field, field),
        out_specs=(field, field, P()),
        check_vma=False,
    )


def solution(mesh):
    return build(mesh, (mesh.shape["gz"] // 8, 4, 2))
```

time: 85.6 us -> 76.1 us (0.89)
  matrix products: 18 us -> 0 us
  Pallas kernels: 0 us -> 8.74 us
  starting transfers between devices: 11.1 us -> 16 us
  other arithmetic: 4.1 us -> 1.18 us
  local copies, waits for them, and re-layouts: 4.64 us -> 6.15 us
  waiting for transfers between devices: 3.42 us -> 2.09 us
  blocking collectives: 41.6 us -> 40.7 us
    psum x4 -> x0, blocking collectives: 41.6 us -> none  [one_axis_at_a_time(): value = lax.psum(value, axis)]
    all_to_all x0 -> x2, blocking collectives: none -> 40.7 us  [the longest x1 22.9 us: shards(): part = lax.all_to_all(part, line_of, 0, 0)]
    dot_general x2 -> x0, matrix products: 18 us -> none  [the longest x1 12.6 us: shards(): jnp.einsum('k,kzyx->zyx', coeff_b, basis, preferred_element_type=jnp.floa...]
    pallas_call x0 -> x3, Pallas kernels: none -> 8.74 us  [the longest x1 4.8 us: update(): pl.pallas_call(stream_kernel, out_shape=(jax.ShapeDtypeStruct(iterate.sha...]
    unnamed x16, local copies, waits for them, and re-layouts: 1.04 us -> 6.13 us
    ppermute x4 -> x8, starting transfers between devices: 11.1 us -> 16 us  [the longest x1 5.01 us: shards(): lax.ppermute(jnp.where(odd == 0, kappa[:, -1], kappa[:, 0]), 'gy', even_y)]
    reshape x2 -> x0, local copies, waits for them, and re-layouts: 2.55 us -> none  [the longest x1 2.47 us: local_sketch(): skewed = doubled[SK:SK + BLK * (2 * SK - 1)].reshape(BLK, 2 * SK - 1)]
    reduce_sum x2 -> x1, other arithmetic: 1.89 us -> 0.02 us  [shards(): part = jnp.broadcast_to(jnp.sum(part, 0), (others, ROWS, BLK))]
  transfers between devices with their start and end apart: 4 -> 8, of which waited for: 2 -> 2; matrix products, arithmetic and copies ran while one was open for 0% -> 0% of each run, Pallas kernels for 0% -> 6%
where the time goes in v1:
time: 76.1 us; the launch traced here: 75.7 us
  blocking collectives  40.7 us (53%)
  starting transfers between devices  16 us (21%)
  Pallas kernels  8.74 us (11%)
  local copies, waits for them, and re-layouts  6.15 us (8%)
  waiting for transfers between devices  2.09 us (3%)
  other arithmetic  1.18 us (2%)
  between operations  0.85 us (1%)
    all_to_all x1, blocking collectives, shards(): part = lax.all_to_all(part, line_of, 0, 0)  22.9 us
    all_to_all x1, blocking collectives, shards(): part = lax.all_to_all(part, plane_of, 0, 0)  17.8 us
    unnamed x16, local copies, waits for them, and re-layouts  6.13 us
    ppermute x1, starting transfers between devices, shards(): lax.ppermute(jnp.where(odd == 0, kappa[:, -1], kappa[:, 0]), 'gy', even_y)  5.01 us
    pallas_call x1, Pallas kernels, update(): pl.pallas_call(stream_kernel, out_shape=(jax.ShapeDtypeStruct(iterate.sha...  4.8 us
    ppermute x1, starting transfers between devices, shards(): k_cross = lax.ppermute(jnp.where(core == 0, kappa[0], kappa[1]), GZ, cross)  4.5 us
    pallas_call x1, Pallas kernels, residual_and_sketch(): pl.pallas_call(residual_kernel, out_shape=(jax.ShapeDtypeStruct(u.shape,...  3.19 us
    ppermute x1, starting transfers between devices, shards(): u_cross = lax.ppermute(u_cross, GZ, cross)  3.02 us
  transfers between devices with their start and end apart: 8, of which 2 were waited for; matrix products, arithmetic and copies ran while one was open for 0% of the time, Pallas kernels for 6%

profile of v1, /device:TPU:1, one launch (start us, length us, event | category | flops | bytes accessed | tf_op | source)
XLA Modules:
  0.0 75.7 jit_solution(15755224861196936989)
XLA Ops:
  0.6 0.0 copy-start.1
  0.6 0.0 copy-start.5
  0.7 0.0 copy-start.3
  0.7 1.2 %select_bitcast_fusion = (f32[64,1024]{1,0:T(8,128)S(1)}, f32[64,1024]{1,0:T(8,128)S(1)}) fusion(f32[2,64,1024]{2,1,0:T(8,128)} %k_ref.1, pred[]{:T(512)S(6)} %eq.8), kind=kLoop, calls=%fused_computation | loop fusion | flops 131072 | bytes 1048577 | tf_op jit(solution)/shard_map/jit(_where)/select_n | solution.py:201
  1.8 4.5 %collective-permute-start.3 = (f32[64,1024]{1,0:T(8,128)S(1)}, f32[64,1024]{1,0:T(8,128)S(1)}, u32[]{:S(2)}, u32[]{:S(2)}) collective-permute-start(f32[64,1024]{1,0:T(8,128)S(1)} %get-tuple-element.19), channel_id=1, source_target_pairs={{4,8},{12,16},{20,24},{28,32},{36,40},{44,48},{52,56},{60,64},{68,... | collective-permute-start | bytes 786440 | tf_op jit(solution)/shard_map/ppermute | solution.py:201
  6.3 0.1 collective-permute-start.2
  6.4 0.0 copy-start
  6.4 3.4 %copy-done = bf16[32,2,64,1024]{3,2,1,0:T(8,128)(2,1)S(1)} copy-done((bf16[32,2,64,1024]{3,2,1,0:T(8,128)(2,1)S(1)}, bf16[32,2,64,1024]{3,2,1,0:T(8,128)(2,1)}, u32[]{:S(2)}) %copy-start) | copy-done | bytes 8388632
  9.8 0.0 copy-start.2
  9.8 1.0 %copy-done.2 = f32[2,64,1024]{2,1,0:T(8,128)S(1)} copy-done((f32[2,64,1024]{2,1,0:T(8,128)S(1)}, f32[2,64,1024]{2,1,0:T(8,128)}, u32[]{:S(2)}) %copy-start.2) | copy-done | bytes 524312
  10.9 0.0 copy-start.7
  10.9 0.7 copy-done.7
  11.5 0.0 copy-start.6
  11.5 4.8 %update.1 = (f32[2,64,1024]{2,1,0:T(8,128)}, f32[64,1024]{1,0:T(8,128)S(1)}, f32[64,1024]{1,0:T(8,128)S(1)}, f32[2,1024]{1,0:T(2,128)S(1)}, f32[2,1024]{1,0:T(2,128)S(1)}) custom-call(f32[1,32]{1,0:T(1,128)S(1)} %bitcast.14, f32[2,64,1024]{2,1,0:T(8,128)S(1)} %copy-done.2, bf16[32,2,64,1024]{3,2,1,0:T(8,128)(2,1)S(1)} %copy-done), custom_call_target="tpu_custom_call" | custom-call | flops 8388608 | bytes 8388608 | tf_op jit(solution)/shard_map/update/pallas_call | solution.py:61
  16.3 0.6 collective-permute-start
  16.9 3.0 %collective-permute-start.1 = (f32[64,1024]{1,0:T(8,128)S(1)}, f32[64,1024]{1,0:T(8,128)S(1)}, u32[]{:S(2)}, u32[]{:S(2)}) collective-permute-start(f32[64,1024]{1,0:T(8,128)S(1)} %get-tuple-element.12), channel_id=1, source_target_pairs={{4,8},{12,16},{20,24},{28,32},{36,40},{44,48},{52,56},{60,64},{68,... | collective-permute-start | bytes 786440 | tf_op jit(solution)/shard_map/ppermute | solution.py:207
  19.9 0.0 copy-done.1
  20.0 0.7 collective-permute-start.7
  20.7 0.0 collective-permute-done.7.ko_ref
  20.7 5.0 %collective-permute-start.6 = (f32[2,1024]{1,0:T(2,128)S(1)}, f32[2,1024]{1,0:T(2,128)S(1)}, u32[]{:S(2)}, u32[]{:S(2)}) collective-permute-start(f32[2,1024]{1,0:T(2,128)S(1)} %get-tuple-element.22), channel_id=1, source_target_pairs={{0,1},{1,0},{2,3},{3,2},{4,5},{5,4},{6,7},{7,6},{8,9},{9,8},{10,11... | collective-permute-start | bytes 24584 | tf_op jit(solution)/shard_map/ppermute | solution.py:203
  25.7 1.0 %collective-permute-done.6.ke_ref = f32[2,1024]{1,0:T(2,128)S(1)} collective-permute-done((f32[2,1024]{1,0:T(2,128)S(1)}, f32[2,1024]{1,0:T(2,128)S(1)}, u32[]{:S(2)}, u32[]{:S(2)}) %collective-permute-start.6) | collective-permute-done | bytes 8224 | tf_op jit(solution)/shard_map/ppermute | solution.py:203
  26.7 1.5 %collective-permute-start.4 = (f32[2,1024]{1,0:T(2,128)S(1)}, f32[2,1024]{1,0:T(2,128)S(1)}, u32[]{:S(2)}, u32[]{:S(2)}) collective-permute-start(f32[2,1024]{1,0:T(2,128)S(1)} %get-tuple-element.13), channel_id=1, source_target_pairs={{0,1},{1,0},{2,3},{3,2},{4,5},{5,4},{6,7},{7,6},{8,9},{9,8},{10,11... | collective-permute-start | bytes 24584 | tf_op jit(solution)/shard_map/ppermute | solution.py:209
  28.2 1.0 %collective-permute-done.4.ue_ref = f32[2,1024]{1,0:T(2,128)S(1)} collective-permute-done((f32[2,1024]{1,0:T(2,128)S(1)}, f32[2,1024]{1,0:T(2,128)S(1)}, u32[]{:S(2)}, u32[]{:S(2)}) %collective-permute-start.4) | collective-permute-done | bytes 8224 | tf_op jit(solution)/shard_map/ppermute | solution.py:209
  29.2 0.7 collective-permute-start.5
  29.9 0.0 collective-permute-done.5.uo_ref
  29.9 0.0 collective-permute-done.3.kc_ref
  29.9 0.0 collective-permute-done.2.ks_ref
  29.9 0.0 collective-permute-done.us_ref
  29.9 0.0 collective-permute-done.1.uc_ref
  29.9 0.0 copy-done.5
  29.9 0.0 copy-done.3
  30.0 0.0 copy-done.6
  30.0 0.0 copy-start.4
  30.0 1.0 %copy-done.4 = f32[2,64,1024]{2,1,0:T(8,128)S(1)} copy-done((f32[2,64,1024]{2,1,0:T(8,128)S(1)}, f32[2,64,1024]{2,1,0:T(8,128)}, u32[]{:S(2)}) %copy-start.4) | copy-done | bytes 524312
  31.0 3.2 %residual.1 = (f32[2,64,1024]{2,1,0:T(8,128)}, f32[16,16,128]{2,1,0:T(8,128)S(1)}) custom-call(f32[2,64,1024]{2,1,0:T(8,128)S(1)} %copy-done.4, f32[2,64,1024]{2,1,0:T(8,128)S(1)} %copy-done.1, f32[2,64,1024]{2,1,0:T(8,128)S(1)} %copy-done.3, s32[2,8,64]{2,1,0:T(8,128)S(1)} %bitcast.12, s32[2,8,64]{2,1,0:T(8,128)S(1)} %bitcast.13, ...), custom_call_target="tpu_custom_call" | custom-call | flops 7864320 | bytes 1048576 | tf_op jit(solution)/shard_map/residual/pallas_call | solution.py:159
  34.2 17.8 %all_to_all.10 = f32[16,16,128]{2,1,0:T(8,128)S(1)} all-to-all(f32[16,16,128]{2,1,0:T(8,128)S(1)} %get-tuple-element.16), channel_id=1, replica_groups=mesh['z'=8,'x'=4,'core'=2,'gy'=4] {'x','gy'}, dimensions={0} | all-to-all | bytes 262144 | tf_op jit(solution)/shard_map/all_to_all | solution.py:220
  52.0 22.9 %all_to_all.11.parts_ref = f32[16,16,128]{2,1,0:T(8,128)S(1)} all-to-all(f32[16,16,128]{2,1,0:T(8,128)S(1)} %broadcast_in_dim.3), channel_id=1, replica_groups=mesh['z'=8,'x'=4,'core'=2,'gy'=4] {'z','core'}, dimensions={0} | all-to-all | bytes 262144 | tf_op jit(solution)/shard_map/all_to_all | solution.py:222
  74.9 0.7 scaled.1
  (4 shorter events, 0.1 us)
Async XLA Ops:
  0.6 19.3 %copy-start.1 = (f32[2,64,1024]{2,1,0:T(8,128)S(1)}, f32[2,64,1024]{2,1,0:T(8,128)}, u32[]{:S(2)}) copy-start(f32[2,64,1024]{2,1,0:T(8,128)} %k_ref.1) | copy-start | bytes 1572868
  0.6 29.3 %copy-start.5 = (s32[2,64,8]{1,2,0:T(8,128)S(1)}, s32[2,64,8]{1,2,0:T(8,128)}, u32[]{:S(2)}) copy-start(s32[2,64,8]{1,2,0:T(8,128)} %param.12) | copy-start | bytes 12292
  0.7 29.3 %copy-start.3 = (f32[2,64,1024]{2,1,0:T(8,128)S(1)}, f32[2,64,1024]{2,1,0:T(8,128)}, u32[]{:S(2)}) copy-start(f32[2,64,1024]{2,1,0:T(8,128)} %rhs_ref.1) | copy-start | bytes 1572868
  1.8 28.1 %collective-permute-start.3 = (f32[64,1024]{1,0:T(8,128)S(1)}, f32[64,1024]{1,0:T(8,128)S(1)}, u32[]{:S(2)}, u32[]{:S(2)}) collective-permute-start(f32[64,1024]{1,0:T(8,128)S(1)} %get-tuple-element.19), channel_id=1, source_target_pairs={{4,8},{12,16},{20,24},{28,32},{36,40},{44,48},{52,56},{60,64},{68,... | collective-permute-start | bytes 786440 | tf_op jit(solution)/shard_map/ppermute | solution.py:201
  6.3 23.6 %collective-permute-start.2 = (f32[64,1024]{1,0:T(8,128)S(1)}, f32[64,1024]{1,0:T(8,128)S(1)}, u32[]{:S(2)}, u32[]{:S(2)}) collective-permute-start(f32[64,1024]{1,0:T(8,128)S(1)} %get-tuple-element.20), channel_id=1, source_target_pairs={{0,4},{4,0},{8,12},{12,8},{16,20},{20,16},{24,28},{28,24},{32,36},... | collective-permute-start | bytes 786440 | tf_op jit(solution)/shard_map/ppermute | solution.py:202
  6.4 3.4 %copy-start = (bf16[32,2,64,1024]{3,2,1,0:T(8,128)(2,1)S(1)}, bf16[32,2,64,1024]{3,2,1,0:T(8,128)(2,1)}, u32[]{:S(2)}) copy-start(bf16[32,2,64,1024]{3,2,1,0:T(8,128)(2,1)} %basis_ref.1) | copy-start | bytes 25165828
  9.8 1.0 %copy-start.2 = (f32[2,64,1024]{2,1,0:T(8,128)S(1)}, f32[2,64,1024]{2,1,0:T(8,128)}, u32[]{:S(2)}) copy-start(f32[2,64,1024]{2,1,0:T(8,128)} %iterate_ref.1) | copy-start | bytes 1572868
  10.9 0.7 copy-start.7
  11.5 18.4 %copy-start.6 = (s32[2,64,8]{1,2,0:T(8,128)S(1)}, s32[2,64,8]{1,2,0:T(8,128)}, u32[]{:S(2)}) copy-start(s32[2,64,8]{1,2,0:T(8,128)} %param.13) | copy-start | bytes 12292
  16.3 13.6 %collective-permute-start = (f32[64,1024]{1,0:T(8,128)S(1)}, f32[64,1024]{1,0:T(8,128)S(1)}, u32[]{:S(2)}, u32[]{:S(2)}) collective-permute-start(f32[64,1024]{1,0:T(8,128)S(1)} %get-tuple-element.11), channel_id=1, source_target_pairs={{0,4},{4,0},{8,12},{12,8},{16,20},{20,16},{24,28},{28,24},{32,36},... | collective-permute-start | bytes 786440 | tf_op jit(solution)/shard_map/ppermute | solution.py:208
  16.9 13.0 %collective-permute-start.1 = (f32[64,1024]{1,0:T(8,128)S(1)}, f32[64,1024]{1,0:T(8,128)S(1)}, u32[]{:S(2)}, u32[]{:S(2)}) collective-permute-start(f32[64,1024]{1,0:T(8,128)S(1)} %get-tuple-element.12), channel_id=1, source_target_pairs={{4,8},{12,16},{20,24},{28,32},{36,40},{44,48},{52,56},{60,64},{68,... | collective-permute-start | bytes 786440 | tf_op jit(solution)/shard_map/ppermute | solution.py:207
  20.0 0.7 collective-permute-start.7
  20.7 6.1 %collective-permute-start.6 = (f32[2,1024]{1,0:T(2,128)S(1)}, f32[2,1024]{1,0:T(2,128)S(1)}, u32[]{:S(2)}, u32[]{:S(2)}) collective-permute-start(f32[2,1024]{1,0:T(2,128)S(1)} %get-tuple-element.22), channel_id=1, source_target_pairs={{0,1},{1,0},{2,3},{3,2},{4,5},{5,4},{6,7},{7,6},{8,9},{9,8},{10,11... | collective-permute-start | bytes 24584 | tf_op jit(solution)/shard_map/ppermute | solution.py:203
  26.7 2.5 %collective-permute-start.4 = (f32[2,1024]{1,0:T(2,128)S(1)}, f32[2,1024]{1,0:T(2,128)S(1)}, u32[]{:S(2)}, u32[]{:S(2)}) collective-permute-start(f32[2,1024]{1,0:T(2,128)S(1)} %get-tuple-element.13), channel_id=1, source_target_pairs={{0,1},{1,0},{2,3},{3,2},{4,5},{5,4},{6,7},{7,6},{8,9},{9,8},{10,11... | collective-permute-start | bytes 24584 | tf_op jit(solution)/shard_map/ppermute | solution.py:209
  29.2 0.7 collective-permute-start.5
  30.0 1.0 %copy-start.4 = (f32[2,64,1024]{2,1,0:T(8,128)S(1)}, f32[2,64,1024]{2,1,0:T(8,128)}, u32[]{:S(2)}) copy-start(f32[2,64,1024]{2,1,0:T(8,128)} %get-tuple-element.7.u_ref) | copy-start | bytes 1572868
